TPU v7x, 256 devices: a whole 4x4x8 slice. The times are simulated.
256 devices in a mesh: dp: 16 (over x, y), mp: 16 (over z, core).
Axes of the slice: x: 4, y: 4, z: 8, core: 2. Of those that a mesh axis runs over, the one named last changes fastest.
Arguments:
- hidden_in: bfloat16 [2048, 4096], P('dp', 'mp'), may hold values from -6 to 6
- lengths: int32 [16], P('dp'), may hold values from 1 to 128
- norm_attn: float32 [4096], replicated, may hold values from 0.25 to 1.75
- q_weight: bfloat16 [4096, 4096], P('dp', 'mp'), may hold values from -0.01171875 to 0.01171875
- k_weight: bfloat16 [4096, 4096], P('dp', 'mp'), may hold values from -0.09375 to 0.09375
- v_weight: bfloat16 [4096, 4096], P('dp', 'mp'), may hold values from -0.09375 to 0.09375
- out_weight_t: bfloat16 [4096, 4096], P('dp', 'mp'), may hold values from -0.09375 to 0.09375
- norm_ffn: float32 [4096], replicated, may hold values from 0.25 to 1.75
- gate_weight: bfloat16 [4096, 10240], P('dp', 'mp'), may hold values from -0.09375 to 0.09375
- up_weight: bfloat16 [4096, 10240], P('dp', 'mp'), may hold values from -0.09375 to 0.09375
- down_weight_t: bfloat16 [4096, 10240], P('dp', 'mp'), may hold values from -0.0625 to 0.0625
- scale_key: float32 [4096], P('mp'), may hold values from 0.25 to 4
- scale_value: float32 [4096], P('mp'), may hold values from 0.1 to 1.9
- scale_ffn: float32 [10240], P('mp'), may hold values from 0.1 to 1.9
- out_grad: bfloat16 [2048, 4096], P('dp'), may hold values from -6 to 6
- position_bias: float32 [64, 128, 128], P('mp'), may hold values from -6 to 256
Outputs:
- block_out: bfloat16 [2048, 4096], P('dp', 'mp')
- input_grad: bfloat16 [2048, 4096], P('dp', 'mp')
- grad_key: float32 [4096], P('mp')
- grad_value: float32 [4096], P('mp')
- grad_ffn: float32 [10240], P('mp')
Inputs may be any that keep to these rules, and one draw needn't show every extreme that they name: Keys of sequence b at positions lengths[b] and beyond are padding.
All inputs are finite; a program needn't handle non-finite values.
Results may differ from a plain program's by a relative error of at most 0.03.
Values may be sent and summed in bfloat16 or wider, within the bound.
A program may use at most 128 MiB of HBM per device.

v0:
```python
import functools
import jax
import jax.numpy as jnp
from jax import lax
from jax.sharding import Mesh
from jax.sharding import PartitionSpec as P

HEAD_DIM = 64
MP = ("mp_0", "mp_1")
DP = ("dp_0", "dp_1")
EPSILON = 1e-06
NEGATIVE = -1e30


def side_by_side(arrays, axis, dim, along):
    ends, at = ([], 0)
    for a in arrays[:-1]:
        at += a.shape[along]
        ends.append(at)
    both = jnp.concatenate(arrays, axis=along)
    return tuple(jnp.split(lax.all_gather(both, axis, axis=dim, tiled=True), ends, axis=along))


def in_blocks(x, dim, devices):
    dims = x.shape
    blocks = x.reshape(*dims[:dim], devices, dims[dim] // devices, *dims[dim + 1 :])
    return jnp.moveaxis(blocks, dim, 0)


def summed_on_arrival(x, axis, dim):
    blocks = in_blocks(x, dim, lax.axis_size(axis))
    arrived = lax.all_to_all(blocks, axis, split_axis=0, concat_axis=0, tiled=True)
    return arrived.astype(jnp.float32).sum(axis=0)


def summed_rows(x, axes, dim):
    far, near = axes
    blocks = in_blocks(x, dim, lax.axis_size(far))
    nearer = summed_on_arrival(blocks, near, dim + 1)
    arrived = lax.all_to_all(
        nearer.astype(jnp.bfloat16), far, split_axis=0, concat_axis=0, tiled=True
    )
    return arrived.astype(jnp.float32).sum(axis=0)


def filled_up(lines, devices):
    spare = -len(lines) % devices
    return jnp.pad(lines, [(0, spare)] + [(0, 0)] * (lines.ndim - 1))


def from_everyone(x, axis):
    copies = jnp.broadcast_to(x, (lax.axis_size(axis), *x.shape))
    return lax.all_to_all(copies, axis, split_axis=0, concat_axis=0, tiled=True)


def laid_out(blocks, dim):
    dims = list(blocks.shape[1:])
    dims[dim] *= blocks.shape[0]
    return jnp.moveaxis(blocks, 0, dim).reshape(dims)


def gather_axes(x, axes, dim):
    far, near = axes
    blocks = from_everyone(from_everyone(x, far), near)
    return laid_out(blocks.swapaxes(0, 1).reshape(-1, *x.shape), dim)


def sum_by_parts(x, axes):
    lines = x.reshape(-1, x.shape[-1])
    own = summed_rows(filled_up(lines, lax.axis_size(axes[0]) * lax.axis_size(axes[1])), axes, 0)
    whole = gather_axes(own.astype(jnp.bfloat16), axes, 0)
    return whole[: len(lines)].reshape(x.shape).astype(jnp.float32)


def of_everyone(x, axis):
    everything = from_everyone(x, axis)
    return jnp.sum(everything, axis=0)


def over_axes(x, axes):
    return functools.reduce(lax.psum, axes, x)


def inverse_rms(values):
    return lax.rsqrt(jnp.mean(values * values, axis=-1, keepdims=True) + EPSILON)


def gelu_tanh(values):
    return jax.nn.gelu(values, approximate=True)


def contract_last(left_side, right_side):
    return lax.dot_general(
        left_side, right_side, (((1,), (1,)), ((), ())), preferred_element_type=jnp.float32
    )


def norm_back(grad_in, values, inverse, gain_vec):
    scaled = grad_in * gain_vec
    correction = (
        values * inverse * inverse * inverse * jnp.mean(scaled * values, axis=-1, keepdims=True)
    )
    return inverse * scaled - correction


def on_device(
    hidden_in,
    lengths,
    norm_attn,
    q_weight,
    k_weight,
    v_weight,
    out_weight_t,
    norm_ffn,
    gate_weight,
    up_weight,
    down_weight_t,
    scale_key,
    scale_value,
    scale_ffn,
    out_grad,
    position_bias,
):
    full_inputs = lax.all_gather(hidden_in, MP, axis=1, tiled=True)
    q_full, k_full, v_full, o_full, gate_full, up_full, down_full = side_by_side(
        (q_weight, k_weight, v_weight, out_weight_t, gate_weight, up_weight, down_weight_t),
        DP,
        0,
        1,
    )
    seq_local = lengths.shape[0]
    tokens_local = full_inputs.shape[0]
    seq_len = tokens_local // seq_local
    heads_local = q_full.shape[1] // HEAD_DIM
    shaped = (seq_local, seq_len, heads_local, HEAD_DIM)
    inputs32 = full_inputs.astype(jnp.float32)
    inv_first = inverse_rms(inputs32)
    normed_first = (inputs32 * inv_first * norm_attn).astype(jnp.bfloat16)
    queries = jnp.dot(normed_first, q_full, preferred_element_type=jnp.float32).astype(jnp.bfloat16)
    key_pre = jnp.dot(normed_first, k_full, preferred_element_type=jnp.float32)
    value_pre = jnp.dot(normed_first, v_full, preferred_element_type=jnp.float32)
    key_rows = (key_pre * scale_key).astype(jnp.bfloat16)
    value_rows = (value_pre * scale_value).astype(jnp.bfloat16)
    q_heads = queries.reshape(shaped)
    k_heads = key_rows.reshape(shaped)
    v_heads = value_rows.reshape(shaped)
    scores = (
        jnp.einsum("bihe,bjhe->bhij", q_heads, k_heads, preferred_element_type=jnp.float32)
        + position_bias[None]
    )
    positions = lax.broadcasted_iota(jnp.int32, (seq_local, seq_len), 1)
    valid_keys = positions < lengths[:, None]
    scores = jnp.where(valid_keys[:, None, None, :], scores, NEGATIVE)
    largest = jnp.max(scores, axis=-1, keepdims=True)
    exponent = jnp.exp(scores - largest)
    attn_probs = exponent / jnp.sum(exponent, axis=-1, keepdims=True)
    probs_low = attn_probs.astype(jnp.bfloat16)
    context = (
        jnp.einsum("bhij,bjhe->bihe", probs_low, v_heads, preferred_element_type=jnp.float32)
        .reshape(tokens_local, -1)
        .astype(jnp.bfloat16)
    )
    attended = sum_by_parts(contract_last(context, o_full).astype(jnp.bfloat16), ("mp_0", "mp_1"))
    first_sum = inputs32 + attended
    inv_second = inverse_rms(first_sum)
    normed_second = (first_sum * inv_second * norm_ffn).astype(jnp.bfloat16)
    gate_proj = jnp.dot(normed_second, gate_full, preferred_element_type=jnp.float32)
    upward = jnp.dot(normed_second, up_full, preferred_element_type=jnp.float32)
    activated, gelu_back = jax.vjp(gelu_tanh, gate_proj)
    product = activated * upward
    hidden = (product * scale_ffn).astype(jnp.bfloat16)
    ffn_share = summed_on_arrival(contract_last(hidden, down_full).astype(jnp.bfloat16), MP, 1)
    share_width = ffn_share.shape[1]
    offset = lax.axis_index(MP) * share_width
    first_share = lax.dynamic_slice_in_dim(first_sum, offset, share_width, 1)
    block_out = (first_share + ffn_share).astype(jnp.bfloat16)
    d_hidden = jnp.dot(out_grad, down_full, preferred_element_type=jnp.float32)
    grad_ffn_part = jnp.sum(d_hidden * product, axis=0)
    d_product = d_hidden * scale_ffn
    d_gate = gelu_back(d_product * upward)[0].astype(jnp.bfloat16)
    d_up = (d_product * activated).astype(jnp.bfloat16)
    d_second = sum_by_parts(
        (contract_last(d_gate, gate_full) + contract_last(d_up, up_full)).astype(jnp.bfloat16),
        ("mp_0", "mp_1"),
    )
    d_first = out_grad.astype(jnp.float32) + norm_back(d_second, first_sum, inv_second, norm_ffn)
    d_context = jnp.dot(
        d_first.astype(jnp.bfloat16), o_full, preferred_element_type=jnp.float32
    ).astype(jnp.bfloat16)
    dc_heads = d_context.reshape(shaped)
    d_probs = jnp.einsum("bihe,bjhe->bhij", dc_heads, v_heads, preferred_element_type=jnp.float32)
    d_scores = (
        attn_probs * (d_probs - jnp.sum(attn_probs * d_probs, axis=-1, keepdims=True))
    ).astype(jnp.bfloat16)
    d_values = jnp.einsum(
        "bhij,bihe->bjhe", probs_low, dc_heads, preferred_element_type=jnp.float32
    ).reshape(tokens_local, -1)
    d_keys = jnp.einsum(
        "bhij,bihe->bjhe", d_scores, q_heads, preferred_element_type=jnp.float32
    ).reshape(tokens_local, -1)
    d_queries = (
        jnp.einsum("bhij,bjhe->bihe", d_scores, k_heads, preferred_element_type=jnp.float32)
        .reshape(tokens_local, -1)
        .astype(jnp.bfloat16)
    )
    grad_key_part = jnp.sum(d_keys * key_pre, axis=0)
    grad_value_part = jnp.sum(d_values * value_pre, axis=0)
    d_key_pre = (d_keys * scale_key).astype(jnp.bfloat16)
    d_value_pre = (d_values * scale_value).astype(jnp.bfloat16)
    attn_term = (
        contract_last(d_queries, q_full)
        + contract_last(d_key_pre, k_full)
        + contract_last(d_value_pre, v_full)
    )
    d_share = summed_on_arrival(attn_term.astype(jnp.bfloat16), MP, 1)
    gain_share = lax.dynamic_slice_in_dim(norm_attn, offset, share_width, 0)
    input_share = lax.dynamic_slice_in_dim(inputs32, offset, share_width, 1)
    first_grad_share = lax.dynamic_slice_in_dim(d_first, offset, share_width, 1)
    scaled_grad = d_share * gain_share
    dot_share = jnp.sum(scaled_grad * input_share, axis=-1, keepdims=True)
    dot_total = of_everyone(dot_share, MP)
    mean_dot = dot_total / inputs32.shape[1]
    cubed = inv_first * inv_first * inv_first
    input_grad = (
        first_grad_share + inv_first * scaled_grad - input_share * cubed * mean_dot
    ).astype(jnp.bfloat16)
    grad_key, grad_value, grad_ffn = (
        over_axes(grad_key_part, DP),
        over_axes(grad_value_part, DP),
        over_axes(grad_ffn_part, DP),
    )
    return (block_out, input_grad, grad_key, grad_value, grad_ffn)


def solution(mesh):
    finer = Mesh(mesh.devices.reshape(4, 4, 8, 2), ("dp_0", "dp_1", "mp_0", "mp_1"))
    placed = (
        P(DP, MP),
        P(DP),
        P(),
        P(DP, MP),
        P(DP, MP),
        P(DP, MP),
        P(DP, MP),
        P(),
        P(DP, MP),
        P(DP, MP),
        P(DP, MP),
        P(MP),
        P(MP),
        P(MP),
        P(DP, None),
        P(MP, None, None),
    )
    return jax.shard_map(
        on_device,
        mesh=finer,
        in_specs=placed,
        out_specs=(P(DP, MP), P(DP, MP), P(MP), P(MP), P(MP)),
        check_vma=False,
    )
```

profile of v0, /device:TPU:1, one launch (start us, length us, event | category | flops | bytes accessed | tf_op | source)
XLA Modules:
  0.0 437.9 jit_solution(16360203652515288852)
XLA Ops:
  15.9 35.3 %all-gather.3.cloned.1.call-done = bf16[128,4096]{1,0:T(8,128)(2,1)} async-done(((bf16[128,256]{1,0:T(8,128)(2,1)}), bf16[128,4096]{1,0:T(8,128)(2,1)}) %all-gather.3.cloned.1.call-update) | async-done | bytes 1048592 | tf_op jit(solution)/shard_map/all_gather | solution.py:124
  53.2 152.8 %all-gather.5.cloned.1.call-done = bf16[4096,2944]{1,0:T(8,128)(2,1)} async-done(((bf16[256,2944]{1,0:T(8,128)(2,1)}), bf16[4096,2944]{1,0:T(8,128)(2,1)}) %all-gather.5.cloned.1.call-update) | async-done | bytes 24117264 | tf_op jit(solution)/shard_map/all_gather | solution.py:21
  206.1 3.1 multiply_convert_fusion.10
  211.6 2.7 multiply_convert_fusion.9
  215.4 2.4 convolution_convert_fusion.1
  218.0 5.0 %all_to_all.55 = bf16[2,8,8,4096]{3,2,1,0:T(8,128)(2,1)S(1)} all-to-all(bf16[2,8,8,4096]{3,2,1,0:T(8,128)(2,1)S(1)} %bitcast.82), channel_id=1, replica_groups=mesh['dp_0'=4,'dp_1'=4,'mp_0'=8,'mp_1'=2] {'mp_1'}, dimensions={0} | all-to-all | bytes 2097152 | tf_op jit(solution)/shard_map/all_to_all | solution.py:32
  223.4 23.3 %all_to_all.56 = bf16[8,8,4096]{2,1,0:T(8,128)(2,1)S(1)} all-to-all(bf16[8,8,4096]{2,1,0:T(8,128)(2,1)S(1)} %reduce_sum.158), channel_id=1, replica_groups=mesh['dp_0'=4,'dp_1'=4,'mp_0'=8,'mp_1'=2] {'mp_0'}, dimensions={0} | all-to-all | bytes 1048576 | tf_op jit(solution)/shard_map/all_to_all | solution.py:40
  246.8 17.5 %all_to_all.57 = bf16[8,8,4096]{2,1,0:T(8,128)(2,1)S(1)} all-to-all(bf16[8,8,4096]{2,1,0:T(8,128)(2,1)S(1)} %broadcast_in_dim.24), channel_id=1, replica_groups=mesh['dp_0'=4,'dp_1'=4,'mp_0'=8,'mp_1'=2] {'mp_0'}, dimensions={0} | all-to-all | bytes 1048576 | tf_op jit(solution)/shard_map/all_to_all | solution.py:53
  264.4 7.5 %all_to_all.58 = bf16[2,8,8,4096]{3,2,1,0:T(8,128)(2,1)S(1)} all-to-all(bf16[2,8,8,4096]{3,2,1,0:T(8,128)(2,1)S(1)} %broadcast_in_dim.25), channel_id=1, replica_groups=mesh['dp_0'=4,'dp_1'=4,'mp_0'=8,'mp_1'=2] {'mp_1'}, dimensions={0} | all-to-all | bytes 2097152 | tf_op jit(solution)/shard_map/all_to_all | solution.py:53
  272.9 3.5 fusion.7
  276.4 3.7 fusion.11
  280.1 3.7 multiply_reduce_fusion.3
  283.8 4.3 fusion.9
  288.2 4.3 fusion.1
  292.5 5.4 %all_to_all.59 = bf16[2,8,8,4096]{3,2,1,0:T(8,128)(2,1)} all-to-all(bf16[2,8,8,4096]{3,2,1,0:T(8,128)(2,1)S(1)} %bitcast.83), channel_id=1, replica_groups=mesh['dp_0'=4,'dp_1'=4,'mp_0'=8,'mp_1'=2] {'mp_1'}, dimensions={0} | all-to-all | bytes 2097152 | tf_op jit(solution)/shard_map/all_to_all | solution.py:32
  297.9 2.4 reduce_sum.162
  300.3 22.1 %all_to_all.60 = bf16[8,8,4096]{2,1,0:T(8,128)(2,1)} all-to-all(bf16[8,8,4096]{2,1,0:T(8,128)(2,1)} %reduce_sum.162), channel_id=1, replica_groups=mesh['dp_0'=4,'dp_1'=4,'mp_0'=8,'mp_1'=2] {'mp_0'}, dimensions={0} | all-to-all | bytes 1048576 | tf_op jit(solution)/shard_map/all_to_all | solution.py:40
  324.3 4.3 all-to-all-start.7
  328.7 4.5 %convolution_convert_fusion = bf16[128,4096]{1,0:T(8,128)(2,1)S(1)} fusion(bf16[4096,2944]{1,0:T(8,128)(2,1)} %all-gather.5.cloned.1.call-done, f32[640]{0:T(1024)S(1)} %copy-done.17, f32[128,640]{1,0:T(8,128)} %copy-done.24, f32[128,640]{1,0:T(8,128)} %copy-done.9), kind=kOutput, calls=%fused_computation.6 | convolution fusion | flops 672514048 | bytes 6949376 | tf_op jit(solution)/shard_map/dot_general | solution.py:93
  334.2 10.9 %all-to-all-done.7 = bf16[8,8,4096]{2,1,0:T(8,128)(2,1)} async-done(((bf16[8,8,4096]{2,1,0:T(8,128)(2,1)}), bf16[8,8,4096]{2,1,0:T(8,128)(2,1)}, u32[]{:S(2)}, u32[]{:S(2)}) %all-to-all-start.7) | async-done | bytes 524320 | tf_op jit(solution)/shard_map/all_to_all | solution.py:53
  346.3 5.5 %all_to_all.61 = bf16[2,8,8,4096]{3,2,1,0:T(8,128)(2,1)} all-to-all(bf16[2,8,8,4096]{3,2,1,0:T(8,128)(2,1)S(1)} %broadcast_in_dim.27), channel_id=1, replica_groups=mesh['dp_0'=4,'dp_1'=4,'mp_0'=8,'mp_1'=2] {'mp_1'}, dimensions={0} | all-to-all | bytes 2097152 | tf_op jit(solution)/shard_map/all_to_all | solution.py:53
  351.8 4.4 %all-to-all-start.4 = ((bf16[16,128,256]{2,1,0:T(8,128)(2,1)}), bf16[16,128,256]{2,1,0:T(8,128)(2,1)}, u32[]{:S(2)}, u32[]{:S(2)}) async-start(bf16[16,128,256]{2,1,0:T(8,128)(2,1)} %bitcast.81), calls=%async_computation.4 | async-start | bytes 2097152 | tf_op jit(solution)/shard_map/all_to_all | solution.py:32
  369.3 2.4 fusion.19
  371.7 2.4 convolution_add_fusion.1
  374.1 2.5 fusion.2
  377.7 6.7 %all-to-all-done.4 = bf16[16,128,256]{2,1,0:T(8,128)(2,1)} async-done(((bf16[16,128,256]{2,1,0:T(8,128)(2,1)}), bf16[16,128,256]{2,1,0:T(8,128)(2,1)}, u32[]{:S(2)}, u32[]{:S(2)}) %all-to-all-start.4) | async-done | bytes 1048608 | tf_op jit(solution)/shard_map/all_to_all | solution.py:32
  384.4 4.2 all-to-all-start.9
  391.1 9.3 %all-reduce.1 = (f32[256]{0:T(256)S(1)}, f32[256]{0:T(256)S(1)}, f32[640]{0:T(1024)S(1)}) all-reduce(f32[256]{0:T(256)S(1)} %get-tuple-element.26, f32[256]{0:T(256)S(1)} %get-tuple-element.25, f32[640]{0:T(1024)S(1)} %get-tuple-element.23), channel_id=1, replica_groups=mesh['dp_0'=4,'dp_1'=4,'mp_0'=8,'mp_1'=2] {'dp_0'}, use_global_device_ids=true, to_apply=%region_15.16 | all-reduce | flops 1152 | bytes 9216 | tf_op jit(solution)/shard_map/psum | solution.py:81
  400.4 8.0 %all-reduce = (f32[256]{0:T(256)}, f32[256]{0:T(256)}, f32[640]{0:T(1024)}) all-reduce(f32[256]{0:T(256)S(1)} %get-tuple-element.8, f32[256]{0:T(256)S(1)} %get-tuple-element.9, f32[640]{0:T(1024)S(1)} %get-tuple-element.10), channel_id=1, replica_groups=mesh['dp_0'=4,'dp_1'=4,'mp_0'=8,'mp_1'=2] {'dp_1'}, use_global_device_ids=true, to_apply=%region_16.17 | all-reduce | flops 1152 | bytes 9216 | tf_op jit(solution)/shard_map/psum | solution.py:81
  409.8 6.0 %all-to-all-done.9 = bf16[16,128,256]{2,1,0:T(8,128)(2,1)} async-done(((bf16[16,128,256]{2,1,0:T(8,128)(2,1)}), bf16[16,128,256]{2,1,0:T(8,128)(2,1)}, u32[]{:S(2)}, u32[]{:S(2)}) %all-to-all-start.9) | async-done | bytes 1048608 | tf_op jit(solution)/shard_map/all_to_all | solution.py:32
  418.8 3.5 all-to-all-start.10
  423.0 6.3 %all-to-all-done.10 = f32[16,128,1]{1,2,0:T(1,128)S(1)} async-done(((f32[16,128,1]{1,2,0:T(1,128)}), f32[16,128,1]{1,2,0:T(1,128)S(1)}, u32[]{:S(2)}, u32[]{:S(2)}) %all-to-all-start.10) | async-done | bytes 8224 | tf_op jit(solution)/shard_map/all_to_all | solution.py:53
  (109 shorter events, 42.5 us)
Async XLA Ops:
  7.2 6.6 %copy-start.10 = (bf16[256,640]{1,0:T(8,128)(2,1)S(1)}, bf16[256,640]{1,0:T(8,128)(2,1)}, u32[]{:S(2)}) copy-start(bf16[256,640]{1,0:T(8,128)(2,1)} %param.26) | copy-start | bytes 983044
  7.2 44.0 %all-gather.3.cloned.1.call-start = ((), (), s32[]{:S(2)}) async-start(), calls=%async_computation.11 | async-start | bytes 1114112 | tf_op jit(solution)/shard_map/all_gather | solution.py:124
  7.9 198.2 %all-gather.5.cloned.1.call-start = ((), (), s32[]{:S(2)}) async-start(), calls=%async_computation.12 | async-start | bytes 25624576 | tf_op jit(solution)/shard_map/all_gather | solution.py:21
  8.9 6.2 %copy-start.11 = (f32[4,128,128]{2,1,0:T(8,128)S(1)}, f32[4,128,128]{2,1,0:T(8,128)}, u32[]{:S(2)}) copy-start(f32[4,128,128]{2,1,0:T(8,128)} %param.31) | copy-start | bytes 786436
  12.7 193.4 %copy-start.18 = (f32[256]{0:T(256)S(1)}, f32[256]{0:T(256)}, u32[]{:S(2)}) copy-start(f32[256]{0:T(256)} %param.28) | copy-start | bytes 3076
  12.7 193.4 %copy-start.23 = (f32[4096]{0:T(1024)S(1)}, f32[4096]{0:T(1024)}, u32[]{:S(2)}) copy-start(f32[4096]{0:T(1024)} %param.18) | copy-start | bytes 49156
  13.8 1.2 copy-start.3
  53.2 158.4 %copy-start.21 = (f32[128]{0:T(128)}, f32[128]{0:T(128)S(1)}, u32[]{:S(2)}) copy-start(f32[128]{0:T(128)S(1)} %get-tuple-element.14) | copy-start | bytes 1540
  206.1 3.2 copy-start
  209.3 5.7 %copy-start.15 = (bf16[128,256]{0,1:T(8,128)(2,1)}, bf16[128,256]{0,1:T(8,128)(2,1)S(1)}, u32[]{:S(2)}) copy-start(bf16[128,256]{0,1:T(8,128)(2,1)S(1)} %copy.85) | copy-start | bytes 196612
  209.3 2.3 copy-start.19
  211.6 2.9 copy-start.7
  214.5 0.8 copy-start.8
  214.7 0.7 copy-start.4
  272.1 0.7 copy-start.14
  276.4 7.4 %copy-start.24 = (f32[128,640]{1,0:T(8,128)}, f32[128,640]{1,0:T(8,128)S(1)}, u32[]{:S(2)}) copy-start(f32[128,640]{1,0:T(8,128)S(1)} %fusion.7) | copy-start | bytes 983044
  276.4 3.7 copy-start.5
  280.1 8.0 %copy-start.9 = (f32[128,640]{1,0:T(8,128)}, f32[128,640]{1,0:T(8,128)S(1)}, u32[]{:S(2)}) copy-start(f32[128,640]{1,0:T(8,128)S(1)} %fusion.11) | copy-start | bytes 983044
  280.1 3.7 copy-start.17
  324.3 20.8 %all-to-all-start.7 = ((bf16[8,8,4096]{2,1,0:T(8,128)(2,1)}), bf16[8,8,4096]{2,1,0:T(8,128)(2,1)}, u32[]{:S(2)}, u32[]{:S(2)}) async-start(bf16[8,8,4096]{2,1,0:T(8,128)(2,1)} %broadcast_in_dim.26), calls=%async_computation.7 | async-start | bytes 1048576 | tf_op jit(solution)/shard_map/all_to_all | solution.py:53
  351.8 32.6 %all-to-all-start.4 = ((bf16[16,128,256]{2,1,0:T(8,128)(2,1)}), bf16[16,128,256]{2,1,0:T(8,128)(2,1)}, u32[]{:S(2)}, u32[]{:S(2)}) async-start(bf16[16,128,256]{2,1,0:T(8,128)(2,1)} %bitcast.81), calls=%async_computation.4 | async-start | bytes 2097152 | tf_op jit(solution)/shard_map/all_to_all | solution.py:32
  356.2 1.8 copy-start.1
  356.2 1.9 copy-start.6
  358.8 1.4 copy-start.2
  360.2 2.8 copy-start.16
  384.4 31.5 %all-to-all-start.9 = ((bf16[16,128,256]{2,1,0:T(8,128)(2,1)}), bf16[16,128,256]{2,1,0:T(8,128)(2,1)}, u32[]{:S(2)}, u32[]{:S(2)}) async-start(bf16[16,128,256]{2,1,0:T(8,128)(2,1)} %bitcast.80), calls=%async_computation.9 | async-start | bytes 2097152 | tf_op jit(solution)/shard_map/all_to_all | solution.py:32
  388.6 2.4 copy-start.12
  388.6 2.4 copy-start.13
  391.0 38.3 %copy-start.20 = (f32[128]{0:T(128)S(1)}, f32[128]{0:T(128)}, u32[]{:S(2)}) copy-start(f32[128]{0:T(128)} %get-tuple-element.13) | copy-start | bytes 1540
  391.0 38.3 %copy-start.22 = (f32[128]{0:T(128)S(1)}, f32[128]{0:T(128)}, u32[]{:S(2)}) copy-start(f32[128]{0:T(128)} %copy-done.21) | copy-start | bytes 1540
  418.8 10.5 %all-to-all-start.10 = ((f32[16,128,1]{1,2,0:T(1,128)}), f32[16,128,1]{1,2,0:T(1,128)S(1)}, u32[]{:S(2)}, u32[]{:S(2)}) async-start(f32[16,128,1]{1,2,0:T(1,128)} %broadcast_in_dim.28), calls=%async_computation.10 | async-start | bytes 16384 | tf_op jit(solution)/shard_map/all_to_all | solution.py:53
Sparse Core Ops, SparseCore 0:
  9.7 41.4 all-gather.2
  53.7 152.3 all-gather.4
where the time goes:
time: 440 us; the launch traced here: 438 us
  waiting for transfers between devices  219 us (50%)
  blocking collectives  104 us (24%)
  matrix products  49.2 us (11%)
  local copies, waits for them, and re-layouts  17.2 us (4%)
  other arithmetic  17.2 us (4%)
  starting transfers between devices  16.6 us (4%)
  between operations  15.3 us (3%)
    all_gather x1, waiting for transfers between devices, side_by_side(): lax.all_gather(both, axis, axis=dim, tiled=True)  153 us
    all_to_all x2, blocking collectives, summed_rows(): lax.all_to_all(nearer.astype(jnp.bfloat16), far, split_axis=0, concat_axi...  45.3 us
    all_gather x1, waiting for transfers between devices, on_device(): full_inputs = lax.all_gather(hidden_in, MP, axis=1, tiled=True)  35.3 us
    all_to_all x3, blocking collectives, from_everyone(): return lax.all_to_all(copies, axis, split_axis=0, concat_axis=0, tiled=True)  30.6 us
    dot_general x7, matrix products, contract_last(): lax.dot_general(left_side, right_side, (((1,), (1,)), ((), ())), preferre...  22.8 us
    psum x2, blocking collectives, over_axes(): return functools.reduce(lax.psum, axes, x)  17.3 us
    all_to_all x2, waiting for transfers between devices, from_everyone(): return lax.all_to_all(copies, axis, split_axis=0, concat_axis=0, tiled=True)  17.2 us
    all_to_all x2, waiting for transfers between devices, summed_on_arrival(): lax.all_to_all(blocks, axis, split_axis=0, concat_axis=0, tiled=True)  12.7 us
  transfers between devices with their start and end apart: 6, of which 6 were waited for; matrix products, arithmetic and copies ran while one was open for 9% of the time, Pallas kernels for 0%

commit v1 on v0

--- a/solution.py
+++ b/solution.py
@@ -121,7 +121,9 @@
     out_grad,
     position_bias,
 ):
-    full_inputs = lax.all_gather(hidden_in, MP, axis=1, tiled=True)
+    full_inputs = jnp.concatenate(
+        lax.all_to_all(jnp.stack([hidden_in] * lax.axis_size(MP)), MP, 0, 0), axis=1
+    )
     q_full, k_full, v_full, o_full, gate_full, up_full, down_full = side_by_side(
         (q_weight, k_weight, v_weight, out_weight_t, gate_weight, up_weight, down_weight_t),
         DP,

time: 440 us -> 418 us (0.950)
  waiting for transfers between devices: 219 us -> 183 us
  blocking collectives: 104 us -> 85.1 us
  local copies, waits for them, and re-layouts: 17.2 us -> 32.9 us
  starting transfers between devices: 16.6 us -> 29.7 us
  other arithmetic: 17.2 us -> 23.3 us
    all_gather x1, waiting for transfers between devices: 153 us -> 115 us  [side_by_side(): lax.all_gather(both, axis, axis=dim, tiled=True)]
    all_gather x1 -> x0, waiting for transfers between devices: 35.3 us -> none  [on_device(): full_inputs = lax.all_gather(hidden_in, MP, axis=1, tiled=True)]
    all_to_all x0 -> x1, waiting for transfers between devices: none -> 27.2 us  [on_device(): lax.all_to_all(jnp.stack([hidden_in] * lax.axis_size(MP)), MP, 0, 0)]
    all_to_all x3 -> x2, blocking collectives: 30.6 us -> 12.3 us  [from_everyone(): return lax.all_to_all(copies, axis, split_axis=0, concat_axis=0, tiled=True)]
    convert_element_type x0 -> x4, local copies, waits for them, and re-layouts: none -> 10.8 us  [the longest x3 7.81 us: on_device(): inputs32 = full_inputs.astype(jnp.float32)]
    all_to_all x0 -> x1, starting transfers between devices: none -> 9.97 us  [on_device(): lax.all_to_all(jnp.stack([hidden_in] * lax.axis_size(MP)), MP, 0, 0)]
    all_to_all x2 -> x3, waiting for transfers between devices: 17.2 us -> 24.7 us  [from_everyone(): return lax.all_to_all(copies, axis, split_axis=0, concat_axis=0, tiled=True)]
    all_to_all x2 -> x3, starting transfers between devices: 7.82 us -> 11.7 us  [from_everyone(): return lax.all_to_all(copies, axis, split_axis=0, concat_axis=0, tiled=True)]
  transfers between devices with their start and end apart: 6 -> 7, of which waited for: 6 -> 7; matrix products, arithmetic and copies ran while one was open for 9% -> 10% of each run, Pallas kernels for 0% -> 0%
where the time goes in v1:
time: 418 us; the launch traced here: 416 us
  waiting for transfers between devices  183 us (44%)
  blocking collectives  85.1 us (20%)
  matrix products  46.3 us (11%)
  local copies, waits for them, and re-layouts  32.9 us (8%)
  starting transfers between devices  29.7 us (7%)
  other arithmetic  23.3 us (6%)
  between operations  15.4 us (4%)
    all_gather x1, waiting for transfers between devices, side_by_side(): lax.all_gather(both, axis, axis=dim, tiled=True)  115 us
    all_to_all x2, blocking collectives, summed_rows(): lax.all_to_all(nearer.astype(jnp.bfloat16), far, split_axis=0, concat_axi...  45.3 us
    all_to_all x1, waiting for transfers between devices, on_device(): lax.all_to_all(jnp.stack([hidden_in] * lax.axis_size(MP)), MP, 0, 0)  27.2 us
    all_to_all x3, waiting for transfers between devices, from_everyone(): return lax.all_to_all(copies, axis, split_axis=0, concat_axis=0, tiled=True)  24.7 us
    dot_general x7, matrix products, contract_last(): lax.dot_general(left_side, right_side, (((1,), (1,)), ((), ())), preferre...  22.6 us
    psum x2, blocking collectives, over_axes(): return functools.reduce(lax.psum, axes, x)  17.1 us
    all_to_all x2, waiting for transfers between devices, summed_on_arrival(): lax.all_to_all(blocks, axis, split_axis=0, concat_axis=0, tiled=True)  16.3 us
    all_to_all x2, blocking collectives, from_everyone(): return lax.all_to_all(copies, axis, split_axis=0, concat_axis=0, tiled=True)  12.3 us
  transfers between devices with their start and end apart: 7, of which 7 were waited for; matrix products, arithmetic and copies ran while one was open for 10% of the time, Pallas kernels for 0%

profile of v1, /device:TPU:1, one launch (start us, length us, event | category | flops | bytes accessed | tf_op | source)
XLA Modules:
  0.0 415.9 jit_solution(3819890919907943725)
XLA Ops:
  15.3 10.0 %all-to-all-start = ((bf16[16,128,256]{2,1,0:T(8,128)(2,1)}), bf16[16,128,256]{2,1,0:T(8,128)(2,1)S(1)}, u32[]{:S(2)}, u32[]{:S(2)}) async-start(bf16[16,128,256]{2,1,0:T(8,128)(2,1)} %stack.2), calls=%async_computation | async-start | bytes 2097152 | tf_op jit(solution)/shard_map/all_to_all | solution.py:125
  26.1 27.2 %all-to-all-done = bf16[16,128,256]{2,1,0:T(8,128)(2,1)S(1)} async-done(((bf16[16,128,256]{2,1,0:T(8,128)(2,1)}), bf16[16,128,256]{2,1,0:T(8,128)(2,1)S(1)}, u32[]{:S(2)}, u32[]{:S(2)}) %all-to-all-start) | async-done | bytes 1048608 | tf_op jit(solution)/shard_map/all_to_all | solution.py:125
  56.8 115.0 %all-gather.2.cloned.1.call-done = bf16[4096,2944]{1,0:T(8,128)(2,1)} async-done(((bf16[256,2944]{1,0:T(8,128)(2,1)}), bf16[4096,2944]{1,0:T(8,128)(2,1)}) %all-gather.2.cloned.1.call-update) | async-done | bytes 24117264 | tf_op jit(solution)/shard_map/all_gather | solution.py:21
  171.7 2.8 multiply_convert_fusion.9
  177.5 2.8 multiply_convert_fusion.10
  183.1 5.0 %all_to_all.60 = bf16[2,8,8,4096]{3,2,1,0:T(8,128)(2,1)S(1)} all-to-all(bf16[2,8,8,4096]{3,2,1,0:T(8,128)(2,1)S(1)} %bitcast.108), channel_id=1, replica_groups=mesh['dp_0'=4,'dp_1'=4,'mp_0'=8,'mp_1'=2] {'mp_1'}, dimensions={0} | all-to-all | bytes 2097152 | tf_op jit(solution)/shard_map/all_to_all | solution.py:32
  188.6 23.3 %all_to_all.61 = bf16[8,8,4096]{2,1,0:T(8,128)(2,1)S(1)} all-to-all(bf16[8,8,4096]{2,1,0:T(8,128)(2,1)S(1)} %reduce_sum.158), channel_id=1, replica_groups=mesh['dp_0'=4,'dp_1'=4,'mp_0'=8,'mp_1'=2] {'mp_0'}, dimensions={0} | all-to-all | bytes 1048576 | tf_op jit(solution)/shard_map/all_to_all | solution.py:40
  212.7 4.1 all-to-all-start.3
  218.8 14.1 %all-to-all-done.3 = bf16[8,8,4096]{2,1,0:T(8,128)(2,1)} async-done(((bf16[8,8,4096]{2,1,0:T(8,128)(2,1)}), bf16[8,8,4096]{2,1,0:T(8,128)(2,1)}, u32[]{:S(2)}, u32[]{:S(2)}) %all-to-all-start.3) | async-done | bytes 524320 | tf_op jit(solution)/shard_map/all_to_all | solution.py:53
  234.0 6.7 %all_to_all.62 = bf16[2,8,8,4096]{3,2,1,0:T(8,128)(2,1)S(1)} all-to-all(bf16[2,8,8,4096]{3,2,1,0:T(8,128)(2,1)S(1)} %broadcast_in_dim.25), channel_id=1, replica_groups=mesh['dp_0'=4,'dp_1'=4,'mp_0'=8,'mp_1'=2] {'mp_1'}, dimensions={0} | all-to-all | bytes 2097152 | tf_op jit(solution)/shard_map/all_to_all | solution.py:53
  245.6 3.0 copy.126
  250.9 3.6 fusion.11
  254.6 3.8 fusion.7
  258.4 4.3 %multiply_reduce_fusion.2 = (f32[640]{0:T(1024)}, f32[128,640]{1,0:T(8,128)S(1)}) fusion(f32[128,640]{1,0:T(8,128)S(1)} %fusion.7, f32[128,640]{1,0:T(8,128)S(1)} %fusion.11, bf16[128,4096]{1,0:T(8,128)(2,1)S(1)} %copy-done.7, bf16[4096,2944]{1,0:T(8,128)(2,1)} %all-gather.2.cloned.1.call-done), kind=kOutput, calls=%fused_computation.71 | convolution fusion | flops 671989120 | bytes 7277056 | tf_op jit(solution)/shard_map/dot_general | solution.py:179
  262.6 4.3 %fusion.9 = f32[128,4096]{1,0:T(8,128)S(1)} fusion(bf16[4096,2944]{1,0:T(8,128)(2,1)} %all-gather.2.cloned.1.call-done, f32[128,640]{1,0:T(8,128)S(1)} %fusion.11, f32[128,640]{1,0:T(8,128)S(1)} %fusion.7, f32[128,640]{1,0:T(8,128)S(1)} %get-tuple-element.29, f32[640]{0:T(1024)S(1)} %copy-done.26), kind=kOutput, calls=%fused_computation.14 | convolution fusion | flops 672890880 | bytes 8325632 | tf_op jit(solution)/shard_map/dot_general | solution.py:93
  267.0 4.3 %fusion.1 = bf16[128,4096]{1,0:T(8,128)(2,1)S(1)} fusion(f32[128,4096]{1,0:T(8,128)S(1)} %fusion.9, bf16[4096,2944]{1,0:T(8,128)(2,1)} %all-gather.2.cloned.1.call-done, f32[128,640]{1,0:T(8,128)S(1)} %get-tuple-element.29, f32[640]{0:T(1024)S(1)} %copy-done.26, f32[128,640]{1,0:T(8,128)S(1)} %fusion.11), kind=kOutput, calls=%fused_computation.4 | convolution fusion | flops 673038336 | bytes 9046528 | tf_op jit(solution)/shard_map/dot_general | solution.py:93
  271.4 5.3 %all_to_all.63 = bf16[2,8,8,4096]{3,2,1,0:T(8,128)(2,1)} all-to-all(bf16[2,8,8,4096]{3,2,1,0:T(8,128)(2,1)S(1)} %bitcast.109), channel_id=1, replica_groups=mesh['dp_0'=4,'dp_1'=4,'mp_0'=8,'mp_1'=2] {'mp_1'}, dimensions={0} | all-to-all | bytes 2097152 | tf_op jit(solution)/shard_map/all_to_all | solution.py:32
  279.1 22.1 %all_to_all.64 = bf16[8,8,4096]{2,1,0:T(8,128)(2,1)} all-to-all(bf16[8,8,4096]{2,1,0:T(8,128)(2,1)} %reduce_sum.162), channel_id=1, replica_groups=mesh['dp_0'=4,'dp_1'=4,'mp_0'=8,'mp_1'=2] {'mp_0'}, dimensions={0} | all-to-all | bytes 1048576 | tf_op jit(solution)/shard_map/all_to_all | solution.py:40
  303.1 4.1 all-to-all-start.8
  308.8 3.1 copy.130
  311.9 2.8 reshape.181
  314.7 4.3 %convolution_convert_fusion = bf16[128,4096]{1,0:T(8,128)(2,1)S(1)} fusion(bf16[4096,2944]{1,0:T(8,128)(2,1)} %all-gather.2.cloned.1.call-done, f32[640]{0:T(1024)S(1)} %copy-done.26, f32[128,640]{1,0:T(8,128)S(1)} %copy-done.35, f32[128,640]{1,0:T(8,128)S(1)} %copy-done.15), kind=kOutput, calls=%fused_computation.6 | convolution fusion | flops 672514048 | bytes 6949376 | tf_op jit(solution)/shard_map/dot_general | solution.py:93
  320.0 5.2 %all-to-all-done.8 = bf16[8,8,4096]{2,1,0:T(8,128)(2,1)} async-done(((bf16[8,8,4096]{2,1,0:T(8,128)(2,1)}), bf16[8,8,4096]{2,1,0:T(8,128)(2,1)}, u32[]{:S(2)}, u32[]{:S(2)}) %all-to-all-start.8) | async-done | bytes 524320 | tf_op jit(solution)/shard_map/all_to_all | solution.py:53
  326.3 5.6 %all_to_all.65 = bf16[2,8,8,4096]{3,2,1,0:T(8,128)(2,1)} all-to-all(bf16[2,8,8,4096]{3,2,1,0:T(8,128)(2,1)S(1)} %broadcast_in_dim.27), channel_id=1, replica_groups=mesh['dp_0'=4,'dp_1'=4,'mp_0'=8,'mp_1'=2] {'mp_1'}, dimensions={0} | all-to-all | bytes 2097152 | tf_op jit(solution)/shard_map/all_to_all | solution.py:53
  332.0 4.5 %all-to-all-start.5 = ((bf16[16,128,256]{2,1,0:T(8,128)(2,1)}), bf16[16,128,256]{2,1,0:T(8,128)(2,1)}, u32[]{:S(2)}, u32[]{:S(2)}) async-start(bf16[16,128,256]{2,1,0:T(8,128)(2,1)} %bitcast.107), calls=%async_computation.5 | async-start | bytes 2097152 | tf_op jit(solution)/shard_map/all_to_all | solution.py:32
  356.0 8.5 %all-to-all-done.5 = bf16[16,128,256]{2,1,0:T(8,128)(2,1)} async-done(((bf16[16,128,256]{2,1,0:T(8,128)(2,1)}), bf16[16,128,256]{2,1,0:T(8,128)(2,1)}, u32[]{:S(2)}, u32[]{:S(2)}) %all-to-all-start.5) | async-done | bytes 1048608 | tf_op jit(solution)/shard_map/all_to_all | solution.py:32
  364.6 3.6 all-to-all-start.10
  369.7 9.2 %all-reduce.1 = (f32[256]{0:T(256)S(1)}, f32[256]{0:T(256)S(1)}, f32[640]{0:T(1024)S(1)}) all-reduce(f32[256]{0:T(256)S(1)} %get-tuple-element.31, f32[256]{0:T(256)S(1)} %get-tuple-element.30, f32[640]{0:T(1024)} %get-tuple-element.28), channel_id=1, replica_groups=mesh['dp_0'=4,'dp_1'=4,'mp_0'=8,'mp_1'=2] {'dp_0'}, use_global_device_ids=true, to_apply=%region_15.16 | all-reduce | flops 1152 | bytes 9216 | tf_op jit(solution)/shard_map/psum | solution.py:81
  379.0 7.9 %all-reduce = (f32[256]{0:T(256)}, f32[256]{0:T(256)}, f32[640]{0:T(1024)}) all-reduce(f32[256]{0:T(256)S(1)} %get-tuple-element.13, f32[256]{0:T(256)S(1)} %get-tuple-element.14, f32[640]{0:T(1024)S(1)} %get-tuple-element.15), channel_id=1, replica_groups=mesh['dp_0'=4,'dp_1'=4,'mp_0'=8,'mp_1'=2] {'dp_1'}, use_global_device_ids=true, to_apply=%region_16.17 | all-reduce | flops 1152 | bytes 9216 | tf_op jit(solution)/shard_map/psum | solution.py:81
  388.2 7.7 %all-to-all-done.10 = bf16[16,128,256]{2,1,0:T(8,128)(2,1)S(1)} async-done(((bf16[16,128,256]{2,1,0:T(8,128)(2,1)}), bf16[16,128,256]{2,1,0:T(8,128)(2,1)S(1)}, u32[]{:S(2)}, u32[]{:S(2)}) %all-to-all-start.10) | async-done | bytes 1048608 | tf_op jit(solution)/shard_map/all_to_all | solution.py:32
  396.9 3.4 all-to-all-start.11
  401.9 5.4 %all-to-all-done.11 = f32[16,128,1]{1,2,0:T(1,128)S(1)} async-done(((f32[16,128,1]{1,2,0:T(1,128)}), f32[16,128,1]{1,2,0:T(1,128)S(1)}, u32[]{:S(2)}, u32[]{:S(2)}) %all-to-all-start.11) | async-done | bytes 8224 | tf_op jit(solution)/shard_map/all_to_all | solution.py:53
  (142 shorter events, 63.6 us)
Async XLA Ops:
  7.2 5.8 %copy-start.16 = (bf16[256,640]{1,0:T(8,128)(2,1)S(1)}, bf16[256,640]{1,0:T(8,128)(2,1)}, u32[]{:S(2)}) copy-start(bf16[256,640]{1,0:T(8,128)(2,1)} %param.26) | copy-start | bytes 983044
  7.2 164.6 %all-gather.2.cloned.1.call-start = ((), (), s32[]{:S(2)}) async-start(), calls=%async_computation.12 | async-start | bytes 25624576 | tf_op jit(solution)/shard_map/all_gather | solution.py:21
  8.2 6.1 %copy-start.19 = (bf16[128,256]{1,0:T(8,128)(2,1)S(1)}, bf16[128,256]{1,0:T(8,128)(2,1)}, u32[]{:S(2)}) copy-start(bf16[128,256]{1,0:T(8,128)(2,1)} %param.16) | copy-start | bytes 196612
  13.1 12.2 %copy-start.17 = (f32[4,128,128]{2,1,0:T(8,128)S(1)}, f32[4,128,128]{2,1,0:T(8,128)}, u32[]{:S(2)}) copy-start(f32[4,128,128]{2,1,0:T(8,128)} %param.31) | copy-start | bytes 786436
  15.3 38.0 %all-to-all-start = ((bf16[16,128,256]{2,1,0:T(8,128)(2,1)}), bf16[16,128,256]{2,1,0:T(8,128)(2,1)S(1)}, u32[]{:S(2)}, u32[]{:S(2)}) async-start(bf16[16,128,256]{2,1,0:T(8,128)(2,1)} %stack.2), calls=%async_computation | async-start | bytes 2097152 | tf_op jit(solution)/shard_map/all_to_all | solution.py:125
  25.3 29.8 %copy-start.22 = (f32[4096]{0:T(1024)S(1)}, f32[4096]{0:T(1024)}, u32[]{:S(2)}) copy-start(f32[4096]{0:T(1024)} %param.18) | copy-start | bytes 49156
  55.1 116.7 %copy-start.29 = (f32[256]{0:T(256)S(1)}, f32[256]{0:T(256)}, u32[]{:S(2)}) copy-start(f32[256]{0:T(256)} %param.27) | copy-start | bytes 3076
  174.6 2.9 copy-start.11
  174.6 2.9 copy-start.27
  177.0 3.3 copy-start.9
  177.2 3.4 copy-start.6
  177.5 3.1 copy-start.24
  180.4 2.7 copy-start.20
  212.7 20.1 %all-to-all-start.3 = ((bf16[8,8,4096]{2,1,0:T(8,128)(2,1)}), bf16[8,8,4096]{2,1,0:T(8,128)(2,1)}, u32[]{:S(2)}, u32[]{:S(2)}) async-start(bf16[8,8,4096]{2,1,0:T(8,128)(2,1)} %broadcast_in_dim.24), calls=%async_computation.3 | async-start | bytes 1048576 | tf_op jit(solution)/shard_map/all_to_all | solution.py:53
  254.6 12.4 %copy-start.14 = (f32[128,640]{1,0:T(8,128)}, f32[128,640]{1,0:T(8,128)S(1)}, u32[]{:S(2)}) copy-start(f32[128,640]{1,0:T(8,128)S(1)} %fusion.11) | copy-start | bytes 983044
  254.6 3.8 copy-start.7
  258.4 4.3 %copy-start.34 = (f32[128,640]{1,0:T(8,128)}, f32[128,640]{1,0:T(8,128)S(1)}, u32[]{:S(2)}) copy-start(f32[128,640]{1,0:T(8,128)S(1)} %fusion.7) | copy-start | bytes 983044
  258.4 4.3 %copy-start.26 = (f32[640]{0:T(1024)S(1)}, f32[640]{0:T(1024)}, u32[]{:S(2)}) copy-start(f32[640]{0:T(1024)} %param.29) | copy-start | bytes 7684
  303.1 22.1 %all-to-all-start.8 = ((bf16[8,8,4096]{2,1,0:T(8,128)(2,1)}), bf16[8,8,4096]{2,1,0:T(8,128)(2,1)}, u32[]{:S(2)}, u32[]{:S(2)}) async-start(bf16[8,8,4096]{2,1,0:T(8,128)(2,1)} %broadcast_in_dim.26), calls=%async_computation.8 | async-start | bytes 1048576 | tf_op jit(solution)/shard_map/all_to_all | solution.py:53
  311.9 2.8 copy-start.15
  311.9 2.8 copy-start.35
  326.3 10.1 %copy-start.1 = (bf16[2,8,8,4096]{3,2,1,0:T(8,128)(2,1)S(1)}, bf16[2,8,8,4096]{3,2,1,0:T(8,128)(2,1)}, u32[]{:S(2)}) copy-start(bf16[2,8,8,4096]{3,2,1,0:T(8,128)(2,1)} %copy-done) | copy-start | bytes 3145732
  332.0 32.6 %all-to-all-start.5 = ((bf16[16,128,256]{2,1,0:T(8,128)(2,1)}), bf16[16,128,256]{2,1,0:T(8,128)(2,1)}, u32[]{:S(2)}, u32[]{:S(2)}) async-start(bf16[16,128,256]{2,1,0:T(8,128)(2,1)} %bitcast.107), calls=%async_computation.5 | async-start | bytes 2097152 | tf_op jit(solution)/shard_map/all_to_all | solution.py:32
  343.1 3.6 copy-start.21
  347.5 2.5 copy-start.30
  350.0 2.5 copy-start.28
  354.9 13.9 %copy-start.13 = (f32[128,256]{1,0:T(8,128)S(1)}, f32[128,256]{1,0:T(8,128)}, u32[]{:S(2)}) copy-start(f32[128,256]{1,0:T(8,128)} %get-tuple-element.23) | copy-start | bytes 393220
  364.6 31.4 %all-to-all-start.10 = ((bf16[16,128,256]{2,1,0:T(8,128)(2,1)}), bf16[16,128,256]{2,1,0:T(8,128)(2,1)S(1)}, u32[]{:S(2)}, u32[]{:S(2)}) async-start(bf16[16,128,256]{2,1,0:T(8,128)(2,1)} %bitcast.97), calls=%async_computation.10 | async-start | bytes 2097152 | tf_op jit(solution)/shard_map/all_to_all | solution.py:32
  368.8 27.4 %copy-start.23 = (f32[256]{0:T(256)S(1)}, f32[256]{0:T(256)}, u32[]{:S(2)}) copy-start(f32[256]{0:T(256)} %dynamic_slice.14) | copy-start | bytes 3076
  368.8 38.6 %copy-start.32 = (f32[128]{0:T(128)S(1)}, f32[128]{0:T(128)}, u32[]{:S(2)}) copy-start(f32[128]{0:T(128)} %copy-done.31) | copy-start | bytes 1540
  369.7 37.6 %copy-start.33 = (f32[128]{0:T(128)S(1)}, f32[128]{0:T(128)}, u32[]{:S(2)}) copy-start(f32[128]{0:T(128)} %get-tuple-element.18) | copy-start | bytes 1540
  396.9 10.4 %all-to-all-start.11 = ((f32[16,128,1]{1,2,0:T(1,128)}), f32[16,128,1]{1,2,0:T(1,128)S(1)}, u32[]{:S(2)}, u32[]{:S(2)}) async-start(f32[16,128,1]{1,2,0:T(1,128)} %broadcast_in_dim.28), calls=%async_computation.11 | async-start | bytes 16384 | tf_op jit(solution)/shard_map/all_to_all | solution.py:53
  (11 other events, 19.8 us)
Sparse Core Ops, SparseCore 0:
  14.3 157.3 all-gather.1
